TPU v7x, 16 devices: a 4x2x1 block of a 4x4x8 slice. The times are simulated.
16 devices in a mesh: dp: 4 (over y, z, core), tp: 4 (over x).
Axes of the slice: x: 4, y: 2, z: 1, core: 2. Of those that a mesh axis runs over, the one named last changes fastest.
The devices are a block of a 4x4x8 slice.
Arguments:
- x: bfloat16 [512, 2048], P('dp'), parts along dimension 0
- w_gate: bfloat16 [2048, 5632], P(None, 'tp')
- w_up: bfloat16 [2048, 5632], P(None, 'tp')
- w_down: bfloat16 [5632, 2048], P('tp')
Outputs:
- output: bfloat16 [512, 2048], P('dp'), parts along dimension 0
There are 4 independent parts. A program takes and returns all parts, laid end to end along the dimension named above; an argument that names none is the same for every part.
All inputs are finite; a program needn't handle non-finite values.
Results may differ from a plain program's by a relative error of at most 0.016.
Values are sent between devices in bfloat16 or wider.
A program may use at most 768 MiB of HBM per device.

v0:
```python
import jax
import jax.numpy as jnp
from jax import lax
from jax.sharding import PartitionSpec as P


def solution(mesh):
    def step(x, w_gate, w_up, w_down):
        gate = jnp.dot(x, w_gate, preferred_element_type=jnp.float32)
        up = jnp.dot(x, w_up, preferred_element_type=jnp.float32)
        hidden = (jax.nn.silu(gate) * up).astype(jnp.bfloat16)
        term = jnp.dot(hidden, w_down, preferred_element_type=jnp.float32).astype(jnp.bfloat16)
        return lax.psum(term, "tp")

    return jax.shard_map(
        step,
        mesh=mesh,
        in_specs=(P("dp", None), P(None, "tp"), P(None, "tp"), P("tp", None)),
        out_specs=P("dp", None),
        check_vma=False,
    )
```

profile of v0, /device:TPU:112, one launch (start us, length us, event | category | flops | bytes accessed | tf_op | source)
XLA Modules:
  0.0 64.7 jit_solution(15197410695595307025)
XLA Ops:
  6.5 0.0 copy-start
  6.6 0.0 all-reduce.2.cloned.1.call-start
  6.6 1.0 %copy-done = bf16[128,2048]{1,0:T(8,128)(2,1)S(1)} copy-done((bf16[128,2048]{1,0:T(8,128)(2,1)S(1)}, bf16[128,2048]{1,0:T(8,128)(2,1)}, u32[]{:S(2)}) %copy-start) | copy-done | bytes 524312
  7.6 3.6 %fusion.3 = f32[128,1408]{1,0:T(8,128)S(1)} fusion(bf16[128,2048]{1,0:T(8,128)(2,1)S(1)} %copy-done, bf16[2048,1408]{1,0:T(8,128)(2,1)} %param.5), kind=kOutput, calls=%fused_computation.5 | convolution fusion | flops 738197504 | bytes 7012352 | tf_op jit(solution)/shard_map/dot_general | solution.py:9
  11.2 7.1 %convolution_convert_fusion = bf16[128,2048]{1,0:T(8,128)(2,1)} fusion(bf16[1408,2048]{1,0:T(8,128)(2,1)} %param.7, bf16[128,2048]{1,0:T(8,128)(2,1)S(1)} %copy-done, bf16[2048,1408]{1,0:T(8,128)(2,1)} %param.6, f32[128,1408]{1,0:T(8,128)S(1)} %fusion.3), kind=kOutput, calls=%fused_computation.2 | convolution fusion | flops 1477738496 | bytes 13303808 | tf_op jit(solution)/shard_map/dot_general | solution.py:12
  18.3 0.1 all-reduce.2.cloned.1.call-update
  18.3 37.7 %all-reduce.2.cloned.1.call-done = bf16[128,2048]{1,0:T(8,128)(2,1)} async-done(((bf16[128,2048]{1,0:T(8,128)(2,1)}), bf16[128,2048]{1,0:T(8,128)(2,1)}) %all-reduce.2.cloned.1.call-update) | async-done | bytes 524304 | tf_op jit(solution)/shard_map/psum | solution.py:13
  56.0 1.9 %copy.6 = bf16[128,2048]{1,0:T(8,128)(2,1)} copy(bf16[128,2048]{1,0:T(8,128)(2,1)} %all-reduce.2.cloned.1.call-done) | data formatting | bytes 1048576
Async XLA Ops:
  6.5 1.0 %copy-start = (bf16[128,2048]{1,0:T(8,128)(2,1)S(1)}, bf16[128,2048]{1,0:T(8,128)(2,1)}, u32[]{:S(2)}) copy-start(bf16[128,2048]{1,0:T(8,128)(2,1)} %param.4) | copy-start | bytes 1572868
  6.6 49.4 %all-reduce.2.cloned.1.call-start = ((), (), s32[]{:S(2)}) async-start(), calls=%async_computation | async-start | bytes 1048576 | tf_op jit(solution)/shard_map/psum | solution.py:13
Sparse Core Ops, SparseCore 0:
  18.5 37.4 all-reduce.1
where the time goes:
time: 64.9 us; the launch traced here: 64.7 us
  waiting for transfers between devices  37.7 us (58%)
  between operations  13.4 us (21%)
  matrix products  10.7 us (16%)
  local copies, waits for them, and re-layouts  2.92 us (4%)
    psum x1, waiting for transfers between devices, step(): return lax.psum(term, 'tp')  37.7 us
    dot_general x1, matrix products, step(): jnp.dot(hidden, w_down, preferred_element_type=jnp.float32)  7.06 us
    dot_general x1, matrix products, step(): gate = jnp.dot(x, w_gate, preferred_element_type=jnp.float32)  3.63 us
    unnamed x3, local copies, waits for them, and re-layouts  2.92 us
  transfers between devices with their start and end apart: 1, of which 1 were waited for; matrix products, arithmetic and copies ran while one was open for 0% of the time, Pallas kernels for 0%

commit v1 on v0

v1 whole, which is shorter than its diff:
```python
import functools

import jax
import jax.numpy as jnp
from jax import lax
from jax.experimental import pallas as pl
from jax.experimental.pallas import tpu as pltpu
from jax.sharding import PartitionSpec as P

MESH = pl.DeviceIdType.MESH
BLOCK = 256
SUBS = 2


def blocks(total, size):
    return [(at, min(size, total - at)) for at in range(0, total, size)]


def kernel(n, x_hbm, wg_hbm, wu_hbm, wd_hbm, y_ref, x_ref, wg, wu, wd, hidden, own, out_buf, in_buf,
           x_sem, gu_sem, wd_sem, send_sem, recv_sem, gather_send, gather_recv):
    me = lax.axis_index("tp")
    chunk = y_ref.shape[1] // n
    width = chunk // SUBS
    hops = [2, 1, 3, 0]

    def peer(hop):
        return lax.rem(me + hop, n)

    def columns(hop, sub):
        return pl.ds(pl.multiple_of(peer(hop) * chunk + sub * width, width), width)

    barrier = pltpu.get_barrier_semaphore()
    for hop in range(1, n):
        pl.semaphore_signal(barrier, inc=1, device_id={"tp": peer(hop)}, device_id_type=MESH)

    x_copy = pltpu.make_async_copy(x_hbm, x_ref, x_sem)
    x_copy.start()
    gu_copies = []
    for i, (at, size) in enumerate(blocks(hidden.shape[1], BLOCK)):
        cut = pl.ds(at, size)
        pair = [
            pltpu.make_async_copy(wg_hbm.at[:, cut], wg.at[:, cut], gu_sem.at[0, i]),
            pltpu.make_async_copy(wu_hbm.at[:, cut], wu.at[:, cut], gu_sem.at[1, i]),
        ]
        for copy in pair:
            copy.start()
        gu_copies.append(pair)
    wd_copies = {}
    for hop in hops:
        for sub in range(SUBS):
            copy = pltpu.make_async_copy(wd_hbm.at[:, columns(hop, sub)], wd.at[hop, sub], wd_sem.at[hop, sub])
            copy.start()
            wd_copies[hop, sub] = copy

    x_copy.wait()
    for (at, size), pair in zip(blocks(hidden.shape[1], BLOCK), gu_copies):
        cut = pl.ds(at, size)
        for copy in pair:
            copy.wait()
        gate = jnp.dot(x_ref[...], wg[:, cut], preferred_element_type=jnp.float32)
        up = jnp.dot(x_ref[...], wu[:, cut], preferred_element_type=jnp.float32)
        hidden[:, cut] = (jax.nn.silu(gate) * up).astype(jnp.bfloat16)

    pl.semaphore_wait(barrier, n - 1)

    terms = {}
    for hop in hops:
        for sub in range(SUBS):
            wd_copies[hop, sub].wait()
            term = jnp.dot(hidden[...], wd[hop, sub], preferred_element_type=jnp.float32)
            if hop == 0:
                own[sub] = term
                continue
            out_buf[hop - 1, sub] = term.astype(jnp.bfloat16)
            copy = pltpu.make_async_remote_copy(
                src_ref=out_buf.at[hop - 1, sub],
                dst_ref=in_buf.at[hop - 1, sub],
                send_sem=send_sem.at[hop - 1, sub],
                recv_sem=recv_sem.at[hop - 1, sub],
                device_id={"tp": peer(hop)},
                device_id_type=MESH,
            )
            copy.start()
            terms[hop, sub] = copy

    gathers = []
    for sub in range(SUBS):
        total = own[sub]
        for hop in hops[:-1]:
            terms[hop, sub].wait_recv()
            total += in_buf[hop - 1, sub].astype(jnp.float32)
        y_ref[:, columns(0, sub)] = total.astype(y_ref.dtype)
        for hop in hops[:-1]:
            copy = pltpu.make_async_remote_copy(
                src_ref=y_ref.at[:, columns(0, sub)],
                dst_ref=y_ref.at[:, columns(0, sub)],
                send_sem=gather_send.at[hop - 1, sub],
                recv_sem=gather_recv.at[hop - 1, sub],
                device_id={"tp": peer(hop)},
                device_id_type=MESH,
            )
            copy.start()
            gathers.append(copy)
    for copy in gathers:
        copy.wait_recv()
    for copy in list(terms.values()) + gathers:
        copy.wait_send()


def solution(mesh):
    n = mesh.shape["tp"]

    def step(x, w_gate, w_up, w_down):
        rows, depth = x.shape
        units, cols = w_down.shape
        width = cols // n // SUBS
        steps = len(blocks(units, BLOCK))
        dma = pltpu.SemaphoreType.DMA
        return pl.pallas_call(
            functools.partial(kernel, n),
            out_shape=pltpu.VMEM((rows, cols), jnp.bfloat16),
            in_specs=[pl.BlockSpec(memory_space=pl.ANY)] * 4,
            out_specs=pl.BlockSpec(memory_space=pltpu.VMEM),
            scratch_shapes=[
                pltpu.VMEM((rows, depth), jnp.bfloat16),
                pltpu.VMEM((depth, units), jnp.bfloat16),
                pltpu.VMEM((depth, units), jnp.bfloat16),
                pltpu.VMEM((n, SUBS, units, width), jnp.bfloat16),
                pltpu.VMEM((rows, units), jnp.bfloat16),
                pltpu.VMEM((SUBS, rows, width), jnp.float32),
                pltpu.VMEM((n - 1, SUBS, rows, width), jnp.bfloat16),
                pltpu.VMEM((n - 1, SUBS, rows, width), jnp.bfloat16),
                dma,
                dma((2, steps)),
                dma((n, SUBS)),
                dma((n - 1, SUBS)),
                dma((n - 1, SUBS)),
                dma((n - 1, SUBS)),
                dma((n - 1, SUBS)),
            ],
            compiler_params=pltpu.CompilerParams(collective_id=0, has_side_effects=True),
        )(x, w_gate, w_up, w_down)

    return jax.shard_map(
        step,
        mesh=mesh,
        in_specs=(P("dp", None), P(None, "tp"), P(None, "tp"), P("tp", None)),
        out_specs=P("dp", None),
        check_vma=False,
    )
```

time: 64.9 us -> 26.5 us (0.41)
  waiting for transfers between devices: 37.7 us -> 0 us
  Pallas kernels: 0 us -> 25.6 us
  between operations: 13.4 us -> 0.01 us
  matrix products: 10.7 us -> 0 us
  local copies, waits for them, and re-layouts: 2.92 us -> 0.8 us
    psum x1 -> x0, waiting for transfers between devices: 37.7 us -> none  [step(): return lax.psum(term, 'tp')]
    pallas_call x0 -> x1, Pallas kernels: none -> 25.6 us  [step(): pl.pallas_call(functools.partial(kernel, n), out_shape=pltpu.VMEM((rows,...]
    dot_general x2 -> x0, matrix products: 10.7 us -> none  [the longest x1 7.06 us: step(): jnp.dot(hidden, w_down, preferred_element_type=jnp.float32)]
    unnamed x3 -> x1, local copies, waits for them, and re-layouts: 2.92 us -> 0.8 us
  transfers between devices with their start and end apart: 1 -> 0, of which waited for: 1 -> 0; matrix products, arithmetic and copies ran while one was open for 0% -> 0% of each run, Pallas kernels for 0% -> 0%
where the time goes in v1:
time: 26.5 us; the launch traced here: 26.4 us
  Pallas kernels  25.6 us (97%)
  local copies, waits for them, and re-layouts  0.8 us (3%)
    pallas_call x1, Pallas kernels, step(): pl.pallas_call(functools.partial(kernel, n), out_shape=pltpu.VMEM((rows,...  25.6 us
    unnamed x1, local copies, waits for them, and re-layouts  0.8 us

profile of v1, /device:TPU:112, one launch (start us, length us, event | category | flops | bytes accessed | tf_op | source)
XLA Modules:
  0.0 26.4 jit_solution(14470399540528011108)
XLA Ops:
  0.0 25.6 %shard_map.46 = bf16[128,2048]{1,0:T(8,128)(2,1)S(1)} custom-call(bf16[128,2048]{1,0:T(8,128)(2,1)} %x_hbm.1, bf16[2048,1408]{1,0:T(8,128)(2,1)} %wg_hbm.1, bf16[2048,1408]{1,0:T(8,128)(2,1)} %wu_hbm.1, bf16[1408,2048]{1,0:T(8,128)(2,1)} %wd_hbm.1), custom_call_target="tpu_custom_call" | custom-call | tf_op jit(solution)/shard_map/pallas_call | solution.py:119
  25.6 0.8 %copy.6 = bf16[128,2048]{1,0:T(8,128)(2,1)} copy(bf16[128,2048]{1,0:T(8,128)(2,1)S(1)} %shard_map.46) | data formatting | bytes 1048576

commit v2 on v1

--- a/solution.py
+++ b/solution.py
@@ -17,7 +17,7 @@
 
 
 def kernel(n, x_hbm, wg_hbm, wu_hbm, wd_hbm, y_ref, x_ref, wg, wu, wd, hidden, own, out_buf, in_buf,
-           x_sem, gu_sem, wd_sem, send_sem, recv_sem, gather_send, gather_recv):
+           x_sem, gu_sem, wd_sem, send_sem, recv_sem, gather_send, gather_recv, order_sem):
     me = lax.axis_index("tp")
     chunk = y_ref.shape[1] // n
     width = chunk // SUBS
@@ -26,15 +26,15 @@
     def peer(hop):
         return lax.rem(me + hop, n)
 
+    def in_order():
+        pl.semaphore_signal(order_sem, inc=1)
+
     def columns(hop, sub):
         return pl.ds(pl.multiple_of(peer(hop) * chunk + sub * width, width), width)
 
-    barrier = pltpu.get_barrier_semaphore()
-    for hop in range(1, n):
-        pl.semaphore_signal(barrier, inc=1, device_id={"tp": peer(hop)}, device_id_type=MESH)
-
     x_copy = pltpu.make_async_copy(x_hbm, x_ref, x_sem)
     x_copy.start()
+    in_order()
     gu_copies = []
     for i, (at, size) in enumerate(blocks(hidden.shape[1], BLOCK)):
         cut = pl.ds(at, size)
@@ -44,13 +44,20 @@
         ]
         for copy in pair:
             copy.start()
+        in_order()
         gu_copies.append(pair)
     wd_copies = {}
     for hop in hops:
         for sub in range(SUBS):
             copy = pltpu.make_async_copy(wd_hbm.at[:, columns(hop, sub)], wd.at[hop, sub], wd_sem.at[hop, sub])
             copy.start()
+            in_order()
             wd_copies[hop, sub] = copy
+    pl.semaphore_wait(order_sem, 1 + len(gu_copies) + len(wd_copies))
+
+    barrier = pltpu.get_barrier_semaphore()
+    for hop in range(1, n):
+        pl.semaphore_signal(barrier, inc=1, device_id={"tp": peer(hop)}, device_id_type=MESH)
 
     x_copy.wait()
     for (at, size), pair in zip(blocks(hidden.shape[1], BLOCK), gu_copies):
@@ -137,6 +144,7 @@
                 dma((n - 1, SUBS)),
                 dma((n - 1, SUBS)),
                 dma((n - 1, SUBS)),
+                pltpu.SemaphoreType.REGULAR,
             ],
             compiler_params=pltpu.CompilerParams(collective_id=0, has_side_effects=True),
         )(x, w_gate, w_up, w_down)

time: 26.5 us -> 23 us (0.87)
  Pallas kernels: 25.6 us -> 22.2 us
    pallas_call x1, Pallas kernels: 25.6 us -> 22.2 us  [step(): pl.pallas_call(functools.partial(kernel, n), out_shape=pltpu.VMEM((rows,...]
where the time goes in v2:
time: 23 us
  Pallas kernels  22.2 us (97%)
  local copies, waits for them, and re-layouts  0.8 us (3%)
    pallas_call x1, Pallas kernels, step(): pl.pallas_call(functools.partial(kernel, n), out_shape=pltpu.VMEM((rows,...  22.2 us
    unnamed x1, local copies, waits for them, and re-layouts  0.8 us

profile of v2, /device:TPU:112, one launch (start us, length us, event | category | flops | bytes accessed | tf_op | source)
XLA Modules:
  0.0 23.0 jit_solution(6867963113969322729)
XLA Ops:
  0.0 22.2 %shard_map.46 = bf16[128,2048]{1,0:T(8,128)(2,1)S(1)} custom-call(bf16[128,2048]{1,0:T(8,128)(2,1)} %x_hbm.1, bf16[2048,1408]{1,0:T(8,128)(2,1)} %wg_hbm.1, bf16[2048,1408]{1,0:T(8,128)(2,1)} %wu_hbm.1, bf16[1408,2048]{1,0:T(8,128)(2,1)} %wd_hbm.1), custom_call_target="tpu_custom_call" | custom-call | tf_op jit(solution)/shard_map/pallas_call | solution.py:126
  22.2 0.8 %copy.6 = bf16[128,2048]{1,0:T(8,128)(2,1)} copy(bf16[128,2048]{1,0:T(8,128)(2,1)S(1)} %shard_map.46) | data formatting | bytes 1048576

commit v3 on v0

v3 whole, which is shorter than its diff:
```python
import functools

import jax
import jax.numpy as jnp
from jax import lax
from jax.experimental import pallas as pl
from jax.experimental.pallas import tpu as pltpu
from jax.sharding import PartitionSpec as P

MESH = pl.DeviceIdType.MESH
BLOCK = 256
WIDTH = 128
HALVED = 3
WHOLE = 2


def both_sides(kind, pieces, *events):
    return [(*event, side, kind, i) for i in range(pieces) for event in [[e] for e in events] or [[]] for side in (0, 1)]


def merge(one, other):
    return [item for pair in zip(one, other) for item in pair] + one[len(other) :] + other[len(one) :]


STEPS = [(side, kind, 0, n) for kind, n in (("other", HALVED), ("kept", HALVED), ("whole", WHOLE)) for side in (0, 1)]
EVENTS = (
    both_sides("kept", HALVED, "join")
    + merge(both_sides("whole", WHOLE, "join"), both_sides("kept", HALVED, "finish"))
    + both_sides("whole", WHOLE, "finish")
)


def blocks(total, size):
    return [(at, min(size, total - at)) for at in range(0, total, size)]


def kernel(n, x_hbm, wg_hbm, wu_hbm, wd_hbm, y_ref, x_ref, wg, wu, wd, hidden, kept, out1, in1, out2, in2,
           x_sem, gu_sem, wd_sem, send1, recv1, send2, recv2, send3, recv3, order_sem):
    me = lax.axis_index("tp")
    span = y_ref.shape[1] // 2
    odd, far = lax.rem(me, 2), n - 1 - me
    near = me + 1 - 2 * odd
    first, second = (near, far), (far, near)
    half = (lax.rem((me + 1) // 2, 2), me // 2)

    def in_order():
        pl.semaphore_signal(order_sem, inc=1)

    def columns(side, kind, piece, pieces=1):
        if kind == "whole":
            return pl.ds(side * span + (2 * HALVED + piece) * WIDTH, pieces * WIDTH)
        at = half[side] if kind == "kept" else 1 - half[side]
        return pl.ds(pl.multiple_of(side * span + (at * HALVED + piece) * WIDTH, WIDTH), pieces * WIDTH)

    def send(src, dst, sends, recvs, to):
        copy = pltpu.make_async_remote_copy(
            src_ref=src, dst_ref=dst, send_sem=sends, recv_sem=recvs, device_id={"tp": to}, device_id_type=MESH
        )
        copy.start()
        return copy

    x_copy = pltpu.make_async_copy(x_hbm, x_ref, x_sem)
    x_copy.start()
    in_order()
    gu_copies = []
    for i, (at, size) in enumerate(blocks(hidden.shape[1], BLOCK)):
        cut = pl.ds(at, size)
        pair = [
            pltpu.make_async_copy(wg_hbm.at[:, cut], wg.at[:, cut], gu_sem.at[0, i]),
            pltpu.make_async_copy(wu_hbm.at[:, cut], wu.at[:, cut], gu_sem.at[1, i]),
        ]
        for copy in pair:
            copy.start()
        in_order()
        gu_copies.append(pair)
    wd_copies, at = [], 0
    for i, (side, kind, piece, pieces) in enumerate(STEPS):
        cut = pl.ds(at, pieces * WIDTH)
        copy = pltpu.make_async_copy(wd_hbm.at[:, columns(side, kind, piece, pieces)], wd.at[:, cut], wd_sem.at[i])
        copy.start()
        in_order()
        wd_copies.append((copy, cut))
        at += pieces * WIDTH
    pl.semaphore_wait(order_sem, 1 + len(gu_copies) + len(wd_copies))

    barrier = pltpu.get_barrier_semaphore()
    for neighbour in first:
        pl.semaphore_signal(barrier, inc=1, device_id={"tp": neighbour}, device_id_type=MESH)

    x_copy.wait()
    for (at, size), pair in zip(blocks(hidden.shape[1], BLOCK), gu_copies):
        cut = pl.ds(at, size)
        for copy in pair:
            copy.wait()
        gate = jnp.dot(x_ref[...], wg[:, cut], preferred_element_type=jnp.float32)
        up = jnp.dot(x_ref[...], wu[:, cut], preferred_element_type=jnp.float32)
        hidden[:, cut] = (jax.nn.silu(gate) * up).astype(jnp.bfloat16)

    pl.semaphore_wait(barrier, 2)

    swaps1, swaps2, swaps3 = {}, {}, {}

    def slot(side, kind, piece):
        return side, piece + (HALVED if kind == "whole" else 0)

    for (side, kind, piece, pieces), (wd_copy, cut) in zip(STEPS, wd_copies):
        wd_copy.wait()
        term = jnp.dot(hidden[...], wd[:, cut], preferred_element_type=jnp.float32)
        for i in range(pieces):
            at = slot(side, kind, piece + i)
            part = term[:, i * WIDTH : (i + 1) * WIDTH]
            if kind == "kept":
                kept[at] = part
            else:
                out1[at] = part.astype(jnp.bfloat16)
        if kind != "kept":
            for i in range(pieces):
                at = slot(side, kind, piece + i)
                swaps1[at] = send(out1.at[at], in1.at[at], send1.at[at], recv1.at[at], first[side])

    for event, side, kind, piece in EVENTS:
        at = slot(side, kind, piece)
        if event == "join":
            swaps1[at].wait_recv()
            mine = kept[at] if kind == "kept" else out1[at].astype(jnp.float32)
            out2[at] = (mine + in1[at].astype(jnp.float32)).astype(jnp.bfloat16)
            swaps2[at] = send(out2.at[at], in2.at[at], send2.at[at], recv2.at[at], second[side])
        else:
            swaps2[at].wait_recv()
            cut = columns(side, kind, piece)
            y_ref[:, cut] = (out2[at].astype(jnp.float32) + in2[at].astype(jnp.float32)).astype(y_ref.dtype)
            if kind == "kept":
                swaps3[at] = send(y_ref.at[:, cut], y_ref.at[:, cut], send3.at[at], recv3.at[at], first[side])
    for copy in swaps3.values():
        copy.wait_recv()
    for copy in [*swaps1.values(), *swaps2.values(), *swaps3.values()]:
        copy.wait_send()


def solution(mesh):
    n = mesh.shape["tp"]
    assert n == 4

    def step(x, w_gate, w_up, w_down):
        rows, depth = x.shape
        units, cols = w_down.shape
        steps = len(blocks(units, BLOCK))
        dma = pltpu.SemaphoreType.DMA
        count = HALVED + WHOLE
        assert cols == 2 * (2 * HALVED + WHOLE) * WIDTH
        pieces = pltpu.VMEM((2, count, rows, WIDTH), jnp.bfloat16)
        return pl.pallas_call(
            functools.partial(kernel, n),
            out_shape=pltpu.VMEM((rows, cols), jnp.bfloat16),
            in_specs=[pl.BlockSpec(memory_space=pl.ANY)] * 4,
            out_specs=pl.BlockSpec(memory_space=pltpu.VMEM),
            scratch_shapes=[
                pltpu.VMEM((rows, depth), jnp.bfloat16),
                pltpu.VMEM((depth, units), jnp.bfloat16),
                pltpu.VMEM((depth, units), jnp.bfloat16),
                pltpu.VMEM((units, cols), jnp.bfloat16),
                pltpu.VMEM((rows, units), jnp.bfloat16),
                pltpu.VMEM((2, HALVED, rows, WIDTH), jnp.float32),
                pieces,
                pieces,
                pieces,
                pieces,
                dma,
                dma((2, steps)),
                dma((len(STEPS),)),
                *[dma((2, count))] * 6,
                pltpu.SemaphoreType.REGULAR,
            ],
            compiler_params=pltpu.CompilerParams(collective_id=0, has_side_effects=True),
        )(x, w_gate, w_up, w_down)

    return jax.shard_map(
        step,
        mesh=mesh,
        in_specs=(P("dp", None), P(None, "tp"), P(None, "tp"), P("tp", None)),
        out_specs=P("dp", None),
        check_vma=False,
    )
```

time: 64.9 us -> 21.3 us (0.33)
  waiting for transfers between devices: 37.7 us -> 0 us
  Pallas kernels: 0 us -> 20.5 us
  between operations: 13.4 us -> 0.01 us
  matrix products: 10.7 us -> 0 us
  local copies, waits for them, and re-layouts: 2.92 us -> 0.8 us
    psum x1 -> x0, waiting for transfers between devices: 37.7 us -> none  [step(): return lax.psum(term, 'tp')]
    pallas_call x0 -> x1, Pallas kernels: none -> 20.5 us  [step(): pl.pallas_call(functools.partial(kernel, n), out_shape=pltpu.VMEM((rows,...]
    dot_general x2 -> x0, matrix products: 10.7 us -> none  [the longest x1 7.06 us: step(): jnp.dot(hidden, w_down, preferred_element_type=jnp.float32)]
    unnamed x3 -> x1, local copies, waits for them, and re-layouts: 2.92 us -> 0.8 us
  transfers between devices with their start and end apart: 1 -> 0, of which waited for: 1 -> 0; matrix products, arithmetic and copies ran while one was open for 0% -> 0% of each run, Pallas kernels for 0% -> 0%
where the time goes in v3:
time: 21.3 us
  Pallas kernels  20.5 us (96%)
  local copies, waits for them, and re-layouts  0.8 us (4%)
    pallas_call x1, Pallas kernels, step(): pl.pallas_call(functools.partial(kernel, n), out_shape=pltpu.VMEM((rows,...  20.5 us
    unnamed x1, local copies, waits for them, and re-layouts  0.8 us

profile of v3, /device:TPU:112, one launch (start us, length us, event | category | flops | bytes accessed | tf_op | source)
XLA Modules:
  0.0 21.3 jit_solution(17473107436159209850)
XLA Ops:
  0.0 20.5 %shard_map.46 = bf16[128,2048]{1,0:T(8,128)(2,1)S(1)} custom-call(bf16[128,2048]{1,0:T(8,128)(2,1)} %x_hbm.1, bf16[2048,1408]{1,0:T(8,128)(2,1)} %wg_hbm.1, bf16[2048,1408]{1,0:T(8,128)(2,1)} %wu_hbm.1, bf16[1408,2048]{1,0:T(8,128)(2,1)} %wd_hbm.1), custom_call_target="tpu_custom_call" | custom-call | tf_op jit(solution)/shard_map/pallas_call | solution.py:152
  20.5 0.8 %copy.6 = bf16[128,2048]{1,0:T(8,128)(2,1)} copy(bf16[128,2048]{1,0:T(8,128)(2,1)S(1)} %shard_map.46) | data formatting | bytes 1048576

commit v4 on v3

--- a/solution.py
+++ b/solution.py
@@ -9,24 +9,26 @@
 
 MESH = pl.DeviceIdType.MESH
 BLOCK = 256
-WIDTH = 128
-HALVED = 3
-WHOLE = 2
+HALVED = (128, 128, 128)
+WHOLE = (256,)
+SIDES = (1, 0)
+GROUPS = (("other", 0, 3), ("kept", 0, 3), ("whole", 0, 1))
 
 
-def both_sides(kind, pieces, *events):
-    return [(*event, side, kind, i) for i in range(pieces) for event in [[e] for e in events] or [[]] for side in (0, 1)]
+def both_sides(kind, event):
+    pieces = WHOLE if kind == "whole" else HALVED
+    return [(event, side, kind, i) for i in range(len(pieces)) for side in SIDES]
 
 
 def merge(one, other):
     return [item for pair in zip(one, other) for item in pair] + one[len(other) :] + other[len(one) :]
 
 
-STEPS = [(side, kind, 0, n) for kind, n in (("other", HALVED), ("kept", HALVED), ("whole", WHOLE)) for side in (0, 1)]
+STEPS = [(side, *group) for group in GROUPS for side in SIDES]
 EVENTS = (
-    both_sides("kept", HALVED, "join")
-    + merge(both_sides("whole", WHOLE, "join"), both_sides("kept", HALVED, "finish"))
-    + both_sides("whole", WHOLE, "finish")
+    both_sides("kept", "join")
+    + merge(both_sides("whole", "join"), both_sides("kept", "finish"))
+    + both_sides("whole", "finish")
 )
 
 
@@ -48,9 +50,10 @@
 
     def columns(side, kind, piece, pieces=1):
         if kind == "whole":
-            return pl.ds(side * span + (2 * HALVED + piece) * WIDTH, pieces * WIDTH)
+            return pl.ds(side * span + 2 * sum(HALVED) + sum(WHOLE[:piece]), sum(WHOLE[piece : piece + pieces]))
         at = half[side] if kind == "kept" else 1 - half[side]
-        return pl.ds(pl.multiple_of(side * span + (at * HALVED + piece) * WIDTH, WIDTH), pieces * WIDTH)
+        at = side * span + at * sum(HALVED) + sum(HALVED[:piece])
+        return pl.ds(pl.multiple_of(at, 128), sum(HALVED[piece : piece + pieces]))
 
     def send(src, dst, sends, recvs, to):
         copy = pltpu.make_async_remote_copy(
@@ -75,12 +78,13 @@
         gu_copies.append(pair)
     wd_copies, at = [], 0
     for i, (side, kind, piece, pieces) in enumerate(STEPS):
-        cut = pl.ds(at, pieces * WIDTH)
-        copy = pltpu.make_async_copy(wd_hbm.at[:, columns(side, kind, piece, pieces)], wd.at[:, cut], wd_sem.at[i])
+        where = columns(side, kind, piece, pieces)
+        cut = pl.ds(at, where.size)
+        copy = pltpu.make_async_copy(wd_hbm.at[:, where], wd.at[:, cut], wd_sem.at[i])
         copy.start()
         in_order()
         wd_copies.append((copy, cut))
-        at += pieces * WIDTH
+        at += where.size
     pl.semaphore_wait(order_sem, 1 + len(gu_copies) + len(wd_copies))
 
     barrier = pltpu.get_barrier_semaphore()
@@ -101,34 +105,37 @@
     swaps1, swaps2, swaps3 = {}, {}, {}
 
     def slot(side, kind, piece):
-        return side, piece + (HALVED if kind == "whole" else 0)
+        return side, piece + (len(HALVED) if kind == "whole" else 0)
 
-    for (side, kind, piece, pieces), (wd_copy, cut) in zip(STEPS, wd_copies):
+    for (side, kind, first_piece, pieces), (wd_copy, cut) in zip(STEPS, wd_copies):
         wd_copy.wait()
         term = jnp.dot(hidden[...], wd[:, cut], preferred_element_type=jnp.float32)
-        for i in range(pieces):
-            at = slot(side, kind, piece + i)
-            part = term[:, i * WIDTH : (i + 1) * WIDTH]
+        at = 0
+        for i in range(first_piece, first_piece + pieces):
+            a, b = slot(side, kind, i)
+            width = (WHOLE if kind == "whole" else HALVED)[i]
+            part = term[:, at : at + width]
+            at += width
             if kind == "kept":
-                kept[at] = part
+                kept[a][b][...] = part
             else:
-                out1[at] = part.astype(jnp.bfloat16)
+                out1[a][b][...] = part.astype(jnp.bfloat16)
         if kind != "kept":
-            for i in range(pieces):
-                at = slot(side, kind, piece + i)
-                swaps1[at] = send(out1.at[at], in1.at[at], send1.at[at], recv1.at[at], first[side])
+            for i in range(first_piece, first_piece + pieces):
+                a, b = at = slot(side, kind, i)
+                swaps1[at] = send(out1[a][b], in1[a][b], send1.at[at], recv1.at[at], first[side])
 
     for event, side, kind, piece in EVENTS:
-        at = slot(side, kind, piece)
+        a, b = at = slot(side, kind, piece)
         if event == "join":
             swaps1[at].wait_recv()
-            mine = kept[at] if kind == "kept" else out1[at].astype(jnp.float32)
-            out2[at] = (mine + in1[at].astype(jnp.float32)).astype(jnp.bfloat16)
-            swaps2[at] = send(out2.at[at], in2.at[at], send2.at[at], recv2.at[at], second[side])
+            mine = kept[a][b][...] if kind == "kept" else out1[a][b][...].astype(jnp.float32)
+            out2[a][b][...] = (mine + in1[a][b][...].astype(jnp.float32)).astype(jnp.bfloat16)
+            swaps2[at] = send(out2[a][b], in2[a][b], send2.at[at], recv2.at[at], second[side])
         else:
             swaps2[at].wait_recv()
             cut = columns(side, kind, piece)
-            y_ref[:, cut] = (out2[at].astype(jnp.float32) + in2[at].astype(jnp.float32)).astype(y_ref.dtype)
+            y_ref[:, cut] = (out2[a][b][...].astype(jnp.float32) + in2[a][b][...].astype(jnp.float32)).astype(y_ref.dtype)
             if kind == "kept":
                 swaps3[at] = send(y_ref.at[:, cut], y_ref.at[:, cut], send3.at[at], recv3.at[at], first[side])
     for copy in swaps3.values():
@@ -146,9 +153,9 @@
         units, cols = w_down.shape
         steps = len(blocks(units, BLOCK))
         dma = pltpu.SemaphoreType.DMA
-        count = HALVED + WHOLE
-        assert cols == 2 * (2 * HALVED + WHOLE) * WIDTH
-        pieces = pltpu.VMEM((2, count, rows, WIDTH), jnp.bfloat16)
+        widths = HALVED + WHOLE
+        assert cols == 2 * (2 * sum(HALVED) + sum(WHOLE))
+        pieces = [[pltpu.VMEM((rows, width), jnp.bfloat16) for width in widths] for side in (0, 1)]
         return pl.pallas_call(
             functools.partial(kernel, n),
             out_shape=pltpu.VMEM((rows, cols), jnp.bfloat16),
@@ -160,7 +167,7 @@
                 pltpu.VMEM((depth, units), jnp.bfloat16),
                 pltpu.VMEM((units, cols), jnp.bfloat16),
                 pltpu.VMEM((rows, units), jnp.bfloat16),
-                pltpu.VMEM((2, HALVED, rows, WIDTH), jnp.float32),
+                [[pltpu.VMEM((rows, width), jnp.float32) for width in HALVED] for side in (0, 1)],
                 pieces,
                 pieces,
                 pieces,
@@ -168,7 +175,7 @@
                 dma,
                 dma((2, steps)),
                 dma((len(STEPS),)),
-                *[dma((2, count))] * 6,
+                *[dma((2, len(widths)))] * 6,
                 pltpu.SemaphoreType.REGULAR,
             ],
             compiler_params=pltpu.CompilerParams(collective_id=0, has_side_effects=True),

time: 21.3 us -> 20.9 us (0.981)
  Pallas kernels: 20.5 us -> 20.1 us
    pallas_call x1, Pallas kernels: 20.5 us -> 20.1 us  [step(): pl.pallas_call(functools.partial(kernel, n), out_shape=pltpu.VMEM((rows,...]
where the time goes in v4:
time: 20.9 us
  Pallas kernels  20.1 us (96%)
  local copies, waits for them, and re-layouts  0.8 us (4%)
    pallas_call x1, Pallas kernels, step(): pl.pallas_call(functools.partial(kernel, n), out_shape=pltpu.VMEM((rows,...  20.1 us
    unnamed x1, local copies, waits for them, and re-layouts  0.8 us

profile of v4, /device:TPU:112, one launch (start us, length us, event | category | flops | bytes accessed | tf_op | source)
XLA Modules:
  0.0 20.9 jit_solution(3386178561962261482)
XLA Ops:
  0.0 20.1 %shard_map.46 = bf16[128,2048]{1,0:T(8,128)(2,1)S(1)} custom-call(bf16[128,2048]{1,0:T(8,128)(2,1)} %x_hbm.1, bf16[2048,1408]{1,0:T(8,128)(2,1)} %wg_hbm.1, bf16[2048,1408]{1,0:T(8,128)(2,1)} %wu_hbm.1, bf16[1408,2048]{1,0:T(8,128)(2,1)} %wd_hbm.1), custom_call_target="tpu_custom_call" | custom-call | tf_op jit(solution)/shard_map/pallas_call | solution.py:159
  20.1 0.8 %copy.6 = bf16[128,2048]{1,0:T(8,128)(2,1)} copy(bf16[128,2048]{1,0:T(8,128)(2,1)S(1)} %shard_map.46) | data formatting | bytes 1048576

commit v5 on v4

--- a/solution.py
+++ b/solution.py
@@ -8,38 +8,35 @@
 from jax.sharding import PartitionSpec as P
 
 MESH = pl.DeviceIdType.MESH
-BLOCK = 256
-HALVED = (128, 128, 128)
-WHOLE = (256,)
+BLOCKS = (384, 512, 256, 256)
+HALVED = ((128, 128, 128), (128, 128, 128))
+WHOLE = ((128,), (384,))
 SIDES = (1, 0)
-GROUPS = (("other", 0, 3), ("kept", 0, 3), ("whole", 0, 1))
+SPANS = [(sum(BLOCKS[:i]), size) for i, size in enumerate(BLOCKS)]
 
 
-def both_sides(kind, event):
-    pieces = WHOLE if kind == "whole" else HALVED
-    return [(event, side, kind, i) for i in range(len(pieces)) for side in SIDES]
+def of_kind(kind, *event):
+    pieces = [(*event, side, kind, i) for side in SIDES for i in range(len((WHOLE if kind == "whole" else HALVED)[side]))]
+    return sorted(pieces, key=lambda piece: piece[-1])
 
 
 def merge(one, other):
     return [item for pair in zip(one, other) for item in pair] + one[len(other) :] + other[len(one) :]
 
 
-STEPS = [(side, *group) for group in GROUPS for side in SIDES]
+STEPS = [
+    (side, kind, 0, len((WHOLE if kind == "whole" else HALVED)[side])) for kind in ("other", "kept", "whole") for side in SIDES
+]
 EVENTS = (
-    both_sides("kept", "join")
-    + merge(both_sides("whole", "join"), both_sides("kept", "finish"))
-    + both_sides("whole", "finish")
+    of_kind("kept", "join")
+    + merge(of_kind("whole", "join"), of_kind("kept", "finish"))
+    + of_kind("whole", "finish")
 )
-
-
-def blocks(total, size):
-    return [(at, min(size, total - at)) for at in range(0, total, size)]
 
 
 def kernel(n, x_hbm, wg_hbm, wu_hbm, wd_hbm, y_ref, x_ref, wg, wu, wd, hidden, kept, out1, in1, out2, in2,
            x_sem, gu_sem, wd_sem, send1, recv1, send2, recv2, send3, recv3, order_sem):
     me = lax.axis_index("tp")
-    span = y_ref.shape[1] // 2
     odd, far = lax.rem(me, 2), n - 1 - me
     near = me + 1 - 2 * odd
     first, second = (near, far), (far, near)
@@ -49,11 +46,14 @@
         pl.semaphore_signal(order_sem, inc=1)
 
     def columns(side, kind, piece, pieces=1):
+        start = side * (2 * sum(HALVED[0]) + sum(WHOLE[0]))
         if kind == "whole":
-            return pl.ds(side * span + 2 * sum(HALVED) + sum(WHOLE[:piece]), sum(WHOLE[piece : piece + pieces]))
+            widths = WHOLE[side]
+            return pl.ds(start + 2 * sum(HALVED[side]) + sum(widths[:piece]), sum(widths[piece : piece + pieces]))
+        widths = HALVED[side]
         at = half[side] if kind == "kept" else 1 - half[side]
-        at = side * span + at * sum(HALVED) + sum(HALVED[:piece])
-        return pl.ds(pl.multiple_of(at, 128), sum(HALVED[piece : piece + pieces]))
+        at = start + at * sum(widths) + sum(widths[:piece])
+        return pl.ds(pl.multiple_of(at, 128), sum(widths[piece : piece + pieces]))
 
     def send(src, dst, sends, recvs, to):
         copy = pltpu.make_async_remote_copy(
@@ -66,7 +66,7 @@
     x_copy.start()
     in_order()
     gu_copies = []
-    for i, (at, size) in enumerate(blocks(hidden.shape[1], BLOCK)):
+    for i, (at, size) in enumerate(SPANS):
         cut = pl.ds(at, size)
         pair = [
             pltpu.make_async_copy(wg_hbm.at[:, cut], wg.at[:, cut], gu_sem.at[0, i]),
@@ -92,7 +92,7 @@
         pl.semaphore_signal(barrier, inc=1, device_id={"tp": neighbour}, device_id_type=MESH)
 
     x_copy.wait()
-    for (at, size), pair in zip(blocks(hidden.shape[1], BLOCK), gu_copies):
+    for (at, size), pair in zip(SPANS, gu_copies):
         cut = pl.ds(at, size)
         for copy in pair:
             copy.wait()
@@ -105,7 +105,7 @@
     swaps1, swaps2, swaps3 = {}, {}, {}
 
     def slot(side, kind, piece):
-        return side, piece + (len(HALVED) if kind == "whole" else 0)
+        return side, piece + (len(HALVED[side]) if kind == "whole" else 0)
 
     for (side, kind, first_piece, pieces), (wd_copy, cut) in zip(STEPS, wd_copies):
         wd_copy.wait()
@@ -113,7 +113,7 @@
         at = 0
         for i in range(first_piece, first_piece + pieces):
             a, b = slot(side, kind, i)
-            width = (WHOLE if kind == "whole" else HALVED)[i]
+            width = (WHOLE if kind == "whole" else HALVED)[side][i]
             part = term[:, at : at + width]
             at += width
             if kind == "kept":
@@ -151,11 +151,11 @@
     def step(x, w_gate, w_up, w_down):
         rows, depth = x.shape
         units, cols = w_down.shape
-        steps = len(blocks(units, BLOCK))
+        assert units == sum(BLOCKS)
         dma = pltpu.SemaphoreType.DMA
-        widths = HALVED + WHOLE
-        assert cols == 2 * (2 * sum(HALVED) + sum(WHOLE))
-        pieces = [[pltpu.VMEM((rows, width), jnp.bfloat16) for width in widths] for side in (0, 1)]
+        widths = [HALVED[side] + WHOLE[side] for side in (0, 1)]
+        assert cols == sum(sum(HALVED[side]) + sum(widths[side]) for side in (0, 1))
+        pieces = [[pltpu.VMEM((rows, width), jnp.bfloat16) for width in widths[side]] for side in (0, 1)]
         return pl.pallas_call(
             functools.partial(kernel, n),
             out_shape=pltpu.VMEM((rows, cols), jnp.bfloat16),
@@ -167,15 +167,15 @@
                 pltpu.VMEM((depth, units), jnp.bfloat16),
                 pltpu.VMEM((units, cols), jnp.bfloat16),
                 pltpu.VMEM((rows, units), jnp.bfloat16),
-                [[pltpu.VMEM((rows, width), jnp.float32) for width in HALVED] for side in (0, 1)],
+                [[pltpu.VMEM((rows, width), jnp.float32) for width in HALVED[side]] for side in (0, 1)],
                 pieces,
                 pieces,
                 pieces,
                 pieces,
                 dma,
-                dma((2, steps)),
+                dma((2, len(BLOCKS))),
                 dma((len(STEPS),)),
-                *[dma((2, len(widths)))] * 6,
+                *[dma((2, max(map(len, widths))))] * 6,
                 pltpu.SemaphoreType.REGULAR,
             ],
             compiler_params=pltpu.CompilerParams(collective_id=0, has_side_effects=True),

time: 20.9 us -> 20.6 us (0.986)
  Pallas kernels: 20.1 us -> 19.8 us
    pallas_call x1, Pallas kernels: 20.1 us -> 19.8 us  [step(): pl.pallas_call(functools.partial(kernel, n), out_shape=pltpu.VMEM((rows,...]
where the time goes in v5:
time: 20.6 us
  Pallas kernels  19.8 us (96%)
  local copies, waits for them, and re-layouts  0.8 us (4%)
    pallas_call x1, Pallas kernels, step(): pl.pallas_call(functools.partial(kernel, n), out_shape=pltpu.VMEM((rows,...  19.8 us
    unnamed x1, local copies, waits for them, and re-layouts  0.8 us

profile of v5, /device:TPU:112, one launch (start us, length us, event | category | flops | bytes accessed | tf_op | source)
XLA Modules:
  0.0 20.6 jit_solution(9978199755502837943)
XLA Ops:
  0.0 19.8 %shard_map.46 = bf16[128,2048]{1,0:T(8,128)(2,1)S(1)} custom-call(bf16[128,2048]{1,0:T(8,128)(2,1)} %x_hbm.1, bf16[2048,1408]{1,0:T(8,128)(2,1)} %wg_hbm.1, bf16[2048,1408]{1,0:T(8,128)(2,1)} %wu_hbm.1, bf16[1408,2048]{1,0:T(8,128)(2,1)} %wd_hbm.1), custom_call_target="tpu_custom_call" | custom-call | tf_op jit(solution)/shard_map/pallas_call | solution.py:159
  19.8 0.8 %copy.6 = bf16[128,2048]{1,0:T(8,128)(2,1)} copy(bf16[128,2048]{1,0:T(8,128)(2,1)S(1)} %shard_map.46) | data formatting | bytes 1048576

commit v6 on v5

--- a/solution.py
+++ b/solution.py
@@ -24,8 +24,8 @@
     return [item for pair in zip(one, other) for item in pair] + one[len(other) :] + other[len(one) :]
 
 
-STEPS = [
-    (side, kind, 0, len((WHOLE if kind == "whole" else HALVED)[side])) for kind in ("other", "kept", "whole") for side in SIDES
+STEPS = [(1, "other", 0, 1), (1, "other", 1, 2), (0, "other", 0, 3)] + [
+    (side, kind, 0, len((WHOLE if kind == "whole" else HALVED)[side])) for kind in ("kept", "whole") for side in SIDES
 ]
 EVENTS = (
     of_kind("kept", "join")
@@ -63,8 +63,6 @@
         return copy
 
     x_copy = pltpu.make_async_copy(x_hbm, x_ref, x_sem)
-    x_copy.start()
-    in_order()
     gu_copies = []
     for i, (at, size) in enumerate(SPANS):
         cut = pl.ds(at, size)
@@ -74,6 +72,8 @@
         ]
         for copy in pair:
             copy.start()
+        if i == 0:
+            x_copy.start()
         in_order()
         gu_copies.append(pair)
     wd_copies, at = [], 0
@@ -85,7 +85,7 @@
         in_order()
         wd_copies.append((copy, cut))
         at += where.size
-    pl.semaphore_wait(order_sem, 1 + len(gu_copies) + len(wd_copies))
+    pl.semaphore_wait(order_sem, len(gu_copies) + len(wd_copies))
 
     barrier = pltpu.get_barrier_semaphore()
     for neighbour in first:

time: 20.6 us -> 20.6 us (level)
  no operation moved by 1% of the time
where the time goes in v6:
time: 20.6 us; the launch traced here: 20.5 us
  Pallas kernels  19.7 us (96%)
  local copies, waits for them, and re-layouts  0.8 us (4%)
    pallas_call x1, Pallas kernels, step(): pl.pallas_call(functools.partial(kernel, n), out_shape=pltpu.VMEM((rows,...  19.7 us
    unnamed x1, local copies, waits for them, and re-layouts  0.8 us

profile of v6, /device:TPU:112, one launch (start us, length us, event | category | flops | bytes accessed | tf_op | source)
XLA Modules:
  0.0 20.5 jit_solution(7897533663048565754)
XLA Ops:
  0.0 19.7 %shard_map.46 = bf16[128,2048]{1,0:T(8,128)(2,1)S(1)} custom-call(bf16[128,2048]{1,0:T(8,128)(2,1)} %x_hbm.1, bf16[2048,1408]{1,0:T(8,128)(2,1)} %wg_hbm.1, bf16[2048,1408]{1,0:T(8,128)(2,1)} %wu_hbm.1, bf16[1408,2048]{1,0:T(8,128)(2,1)} %wd_hbm.1), custom_call_target="tpu_custom_call" | custom-call | tf_op jit(solution)/shard_map/pallas_call | solution.py:159
  19.7 0.8 %copy.6 = bf16[128,2048]{1,0:T(8,128)(2,1)} copy(bf16[128,2048]{1,0:T(8,128)(2,1)S(1)} %shard_map.46) | data formatting | bytes 1048576
